TPU v7x, 256 devices: a whole 4x4x8 slice. The times are simulated.
256 devices in a mesh: dp: 8 (over z), expert: 16 (over y, x), tensor: 2 (over core).
Axes of the slice: x: 4, y: 4, z: 8, core: 2. Of those that a mesh axis runs over, the one named last changes fastest.
Arguments:
- tokens: bfloat16 [1536, 7168], P(('dp', 'expert')), may hold values from -6 to 6
- expert_ids: int32 [1536, 8], P(('dp', 'expert')), may hold values from 0 to 15, all different within a row; in each aligned block of 12 rows (0 to 11, 12 to 23, ...) at most 8 rows name the same one
- route_weights: float32 [1536, 8], P(('dp', 'expert')), may hold values from 0.1 to 1
- gate_weights: bfloat16 [16, 7168, 2048], P('expert', 'dp', 'tensor'), may hold values from -0.0625 to 0.0625
- up_weights: bfloat16 [16, 7168, 2048], P('expert', 'dp', 'tensor'), may hold values from -0.0625 to 0.0625
- down_weights: bfloat16 [16, 2048, 7168], P('expert', 'tensor', 'dp'), may hold values from -0.125 to 0.125
- shared_gate: bfloat16 [7168, 2048], P('dp', 'tensor'), may hold values from -0.0625 to 0.0625
- shared_up: bfloat16 [7168, 2048], P('dp', 'tensor'), may hold values from -0.0625 to 0.0625
- shared_down: bfloat16 [2048, 7168], P('tensor', 'dp'), may hold values from -0.125 to 0.125
Outputs:
- mixed: bfloat16 [1536, 7168], P(('dp', 'expert'))
Inputs may be any that keep to these rules, and one draw needn't show every extreme that they name: `expert_ids`: each token names 8 different experts. In the rows of one device no expert is named by more than 8 tokens, and in some device's rows some expert is named by exactly 8.
All inputs are finite; a program needn't handle non-finite values.
Results may differ from a plain program's by a relative error of at most 0.005.
Values may be sent and summed in bfloat16 or wider, within the bound.
A program may use at most 128 MiB of HBM per device.

v0:
```python
import functools

import jax
import jax.numpy as jnp
from jax import lax
from jax.experimental import pallas as pl
from jax.experimental.pallas import tpu as pltpu
from jax.sharding import PartitionSpec as P

CAP = 8
TP = 16
MESH = pl.DeviceIdType.MESH
F32 = jnp.float32
BF16 = jnp.bfloat16


def dot(a, b):
    return jnp.dot(a, b, preferred_element_type=F32)


def layer_kernel(
    Z, E, T, B, FH,
    ids_ref, rw_ref, tok_hbm, wg_hbm, wu_hbm, wd_hbm, sg_hbm, su_hbm, sd_hbm,
    out_ref,
    wg, wu, wd, sg, su, sd,
    tok, tb, tw, xs, xw, pk, x, p, sb, rb, ssb, srb, hid, hs, acc, os_, orc, sac, sos, sor, oo, rr, fb, ob,
    l_sem, t_sem, a_ss, a_rs, w_ss, w_rs, b_ss, b_rs, f_ss, f_rs,
    c_ss, c_rs, d_ss, d_rs, g_ss, g_rs, h_ss, h_rs, o_ss, o_rs, q_ss, q_rs, r_ss, r_rs, y_ss, y_rs,
):
    H = Z // 2
    NS = E * CAP
    z, e, t = lax.axis_index("dp"), lax.axis_index("expert"), lax.axis_index("tensor")
    zr, zl = lax.rem(z + 1, Z), lax.rem(z + Z - 1, Z)
    far = lax.rem(z + H, Z)
    pt = 1 - t

    barrier = pltpu.get_barrier_semaphore()
    for j in range(1, Z):
        zz = lax.rem(z + j, Z)
        for tt in range(2):
            pl.semaphore_signal(barrier, inc=1, device_id=(zz, e, tt), device_id_type=MESH)
    for j in range(1, E):
        ee = lax.rem(e + j, E)
        pl.semaphore_signal(barrier, inc=1, device_id=(z, ee, t), device_id_type=MESH)
    pl.semaphore_signal(barrier, inc=1, device_id=(z, e, pt), device_id_type=MESH)

    def chunk(i, core):
        return lax.rem(z + (1 - core) * (Z - i) + core * (1 + i), Z)

    def at(way, k):
        return lax.rem(z + Z - k, Z) if way == 0 else lax.rem(z + k, Z)

    def owner_home(way, j):
        return lax.rem(z + Z - j + H, Z) if way == 0 else lax.rem(z + j + H, Z)

    def remote(src, dst, ss, rs, dev):
        return pltpu.make_async_remote_copy(
            src_ref=src, dst_ref=dst, send_sem=ss, recv_sem=rs, device_id=dev, device_id_type=MESH
        )

    def next_to(way):
        return (zr if way == 0 else zl, e, t)

    def take(ref, sem):
        pltpu.make_async_copy(ref, ref, sem).wait()

    def rows(j):
        return pl.ds(pl.multiple_of(j * CAP, CAP), CAP)

    tok_load = pltpu.make_async_copy(tok_hbm, tok, t_sem)
    tok_load.start()
    loads = [
        pltpu.make_async_copy(src, dst, l_sem.at[n])
        for n, (src, dst) in enumerate(
            ((sg_hbm, sg), (su_hbm, su), (wg_hbm, wg), (wu_hbm, wu), (wd_hbm, wd), (sd_hbm, sd))
        )
    ]

    ids = ids_ref[...]
    rw = rw_ref[...]
    slot = lax.broadcasted_iota(jnp.int32, (NS, T), 0)
    named = lax.shift_right_logical(slot, 3)
    m = jnp.zeros((NS, T), F32)
    weight = jnp.zeros((NS, T), F32)
    for k in range(ids.shape[0]):
        hit = ids[k : k + 1, :] == named
        m = m + jnp.where(hit, 1.0, 0.0)
        weight = weight + jnp.where(hit, rw[k : k + 1, :], 0.0)
    token = lax.broadcasted_iota(jnp.int32, (NS, T), 1)
    before = jnp.zeros((NS, T), F32)
    for r in range(T - 1):
        before = before + jnp.where(token > r, m[:, r : r + 1], 0.0)
    placed = jnp.where(before == (slot & 7).astype(F32), weight, 0.0)
    tw[...] = jnp.concatenate([placed, jnp.zeros((NS, NS - T), F32)], axis=1).T[0:TP, :]
    for d in range(Z):
        tb[d, 8:TP, :] = jnp.zeros((TP - 8, B), BF16)
    tok_load.wait()
    for load in loads:
        load.start()
    for d in range(Z):
        tb[d, 0:T, :] = tok[:, d * B : (d + 1) * B]

    pl.semaphore_wait(barrier, 2 * (Z - 1) + (E - 1) + 1)

    def target_a(i):
        return lax.rem(z + (1 - t) * i + t * (Z - 1 - i), Z)

    def copy_a(i, tt):
        return remote(tb.at[target_a(i)], xs.at[z], a_ss.at[i, tt], a_rs.at[t, i], (target_a(i), e, tt))

    def copy_w(i):
        return remote(tw, xw.at[i], w_ss.at[i], w_rs.at[i], (target_a(i), e, t))

    def start_a(i):
        copy_a(i, 0).start()
        copy_a(i, 1).start()
        copy_w(i).start()

    def pick(i):
        zc = chunk(i, t)
        cb = jnp.where(xw[i] > 0.0, 1.0, 0.0).astype(BF16)
        picked = lax.dot_general(cb, xs[zc], (((0,), (0,)), ((), ())), preferred_element_type=F32)
        pk[i] = picked.astype(BF16)

        def send_b(k, carry):
            ee = lax.rem(e + k, E)
            remote(pk.at[i, rows(ee)], x.at[zc, rows(e)], b_ss.at[i], b_rs.at[i], (z, ee, t)).start()
            return carry

        lax.fori_loop(1, E, send_b, 0)
        x[zc, rows(e), :] = pk[i, rows(e), :]

    def copy_d(way, k, half):
        return remote(
            ssb.at[way, k, half], srb.at[way, k, half], d_ss.at[way, k, half], d_rs.at[way, k, half], next_to(way)
        )

    def cols(half):
        return slice(half * FH, (half + 1) * FH)

    def step_s(k):
        for half in range(2):
            ways = (half,) if k == 0 else (0, 1)
            v = [xs[at(way, k)] for way in ways]
            v = v[0] if k == 0 else jnp.concatenate(v, axis=0)
            sums = [dot(v, w[:, cols(half)]) for w in (sg, su)]
            for n, way in enumerate(ways):
                if k > 1 or (k == 1 and half == way):
                    copy_d(way, k - 1, half).wait_recv()
                for q in range(2):
                    u = sums[q][n * TP : (n + 1) * TP]
                    if k > 1 or (k == 1 and half == way):
                        u = u + srb[way, k - 1, half, :, cols(q)].astype(F32)
                    ssb[way, k, half, :, cols(q)] = u.astype(BF16)
                copy_d(way, k, half).start()

    def silu_up(g, u):
        return (g / (1.0 + jnp.exp(-g)) * u).astype(BF16)

    def last_s():
        for half in range(2):
            for way in range(2):
                copy_d(way, H - 1, half).wait_recv()
            g, u = [
                dot(xs[far], w[:, cols(half)])
                + srb[0, H - 1, half, :, cols(q)].astype(F32)
                + srb[1, H - 1, half, :, cols(q)].astype(F32)
                for q, w in enumerate((sg, su))
            ]
            hs[far, half] = silu_up(g, u)

    @pl.when(t == 1)
    def _():
        start_a(0)

    for i in range(1, H):
        start_a(i)
    xs[z] = tb[z]

    @pl.when(t == 0)
    def _():
        xw[0] = tw[...]
        pick(0)

    for load in loads[:2]:
        load.wait()
    step_s(0)
    for k in range(1, H):
        take(xs.at[0], a_rs.at[0, k])
        take(xs.at[0], a_rs.at[1, k - 1])
        take(xw.at[0], w_rs.at[k - t])
        pick(k - t)
        if k == 1 and H > 2:
            step_s(1)
    take(xs.at[0], a_rs.at[1, H - 1])

    @pl.when(t == 1)
    def _():
        take(xw.at[0], w_rs.at[H - 1])
        pick(H - 1)

    for k in range(2, H - 1):
        step_s(k)
    for load in loads[2:4]:
        load.wait()

    def copy_c(way, k, half, q):
        return remote(
            sb.at[way, k, half, q],
            rb.at[way, k, half, q],
            c_ss.at[way, k, half, q],
            c_rs.at[way, k, half, q],
            next_to(way),
        )

    def forward(n):
        zc = chunk(n, t)
        return remote(x.at[zc], x.at[zc], f_ss.at[n], f_rs.at[n], (z, e, pt))

    def pass_on(n):
        take(x.at[chunk(n, t), pl.ds(0, (E - 1) * CAP)], b_rs.at[n])
        forward(n).start()

    def from_partner(n):
        take(x.at[chunk(n, pt)], f_rs.at[n])

    def partial(c, half, q, to):
        p[to, q] = dot(x[c], (wg, wu)[q][:, cols(half)])

    @pl.when(t == 0)
    def _():
        pass_on(0)

    @pl.when(t == 1)
    def _():
        from_partner(0)

    for q in range(2):
        for way in range(2):
            partial(z, way, q, way)
            sb[way, 0, way, q] = p[way, q].astype(BF16)
            copy_c(way, 0, way, q).start()
    step_s(H - 1)

    def step_c(k, carry):
        pass_on(k - t)
        from_partner(k - pt)
        for half in range(2):
            for q in range(2):
                for way in range(2):
                    partial(at(way, k), half, q, way)

                    def plus(half=half, q=q, way=way):
                        copy_c(way, k - 1, half, q).wait_recv()
                        p[way, q] = p[way, q] + rb[way, k - 1, half, q].astype(F32)

                    if half == way:
                        plus()
                    else:
                        pl.when(k > 1)(plus)
                    sb[way, k, half, q] = p[way, q].astype(BF16)
                    copy_c(way, k, half, q).start()
        return carry

    lax.fori_loop(1, H, step_c, 0)

    @pl.when(t == 1)
    def _():
        pass_on(H - 1)

    @pl.when(t == 0)
    def _():
        from_partner(H - 1)

    def copy_g(way, half, j):
        c = owner_home(way, j)
        return remote(
            hid.at[c, half], hid.at[c, half], g_ss.at[way, half, j], g_rs.at[way, half, j], next_to(way)
        )

    def copy_h(way, half, j):
        c = owner_home(way, j)
        return remote(hs.at[c, half], hs.at[c, half], h_ss.at[way, half, j], h_rs.at[way, half, j], next_to(way))

    def hop(copy, way, half, j):
        copy(way, half, j - 1).wait_recv()
        if j < H - 1 or (j == H - 1 and half == way):
            copy(way, half, j).start()

    for half in range(2):
        for q in range(2):
            partial(far, half, q, half)
    last_s()
    for half in range(2):
        for q in range(2):
            for way in range(2):
                copy_c(way, H - 1, half, q).wait_recv()
            p[half, q] = p[half, q] + rb[0, H - 1, half, q].astype(F32) + rb[1, H - 1, half, q].astype(F32)
        hid[far, half] = silu_up(p[half, 0], p[half, 1])
        for way in range(2):
            copy_g(way, half, 0).start()

    for load in loads[4:]:
        load.wait()

    def down(v, w):
        return dot(v[0], w[0:FH, :]) + dot(v[1], w[FH : 2 * FH, :])

    def copy_o(i):
        return remote(os_.at[i], orc.at[i], o_ss.at[i], o_rs.at[i], (z, e, pt))

    def copy_q(i):
        return remote(sos.at[i], sor.at[i], q_ss.at[i], q_rs.at[i], (z, e, pt))

    def keep_or_give(i, keeper, c):
        @pl.when(t == keeper)
        def _():
            acc[i] = down(hid[c], wd)

        @pl.when(t != keeper)
        def _():
            os_[i] = down(hid[c], wd)
            copy_o(i).start()

    def shared_one(i, keeper, c):
        v = down(hs[c], sd)

        @pl.when(t == keeper)
        def _():
            sac[i] = v

        @pl.when(t != keeper)
        def _():
            sos[i] = v
            copy_q(i).start()

    def shared_pair(theirs, mine):
        v = jnp.concatenate([hs[chunk(theirs, pt)], hs[chunk(mine, t)]], axis=1)
        v = down(v, sd)
        sos[theirs] = v[0:TP]
        copy_q(theirs).start()
        sac[mine] = v[TP : 2 * TP]

    def finish(i):
        copy_o(i).wait_recv()
        oo[i] = acc[i] + orc[i]

        def send_r(k, carry):
            ee = lax.rem(e + k, E)
            remote(oo.at[i, rows(ee)], rr.at[i, rows(e)], r_ss.at[i], r_rs.at[i], (z, ee, t)).start()
            return carry

        lax.fori_loop(1, E, send_r, 0)
        rr[i, rows(e), :] = oo[i, rows(e), :]

    keep_or_give(H - 1, 1, far)
    for j in range(1, H):
        mine = H - j - t
        theirs = H - j - pt
        for way in range(2):
            hop(copy_g, way, 0, j)
        if j > 1:
            finish(mine + 1)
        for way in range(2):
            hop(copy_g, way, 1, j)
        for half in range(2):
            for way in range(2):
                if j == 1:
                    copy_h(way, half, 0).start()
                else:
                    hop(copy_h, way, half, j - 1)
        os_[theirs] = down(hid[chunk(theirs, pt)], wd)
        copy_o(theirs).start()
        acc[mine] = down(hid[chunk(mine, t)], wd)
        if j == 1:
            shared_one(H - 1, 1, far)

            @pl.when(t == 1)
            def _():
                finish(H - 1)

        else:
            shared_pair(theirs + 1, mine + 1)
    finish(1 - t)
    for half in range(2):
        for way in range(2):
            hop(copy_h, way, half, H - 1)
    copy_g(0, 0, H - 1).wait_recv()
    copy_g(1, 1, H - 1).wait_recv()
    keep_or_give(0, 0, z)
    shared_pair(1 - pt, 1 - t)

    @pl.when(t == 0)
    def _():
        finish(0)

    copy_h(0, 0, H - 1).wait_recv()
    copy_h(1, 1, H - 1).wait_recv()
    shared_one(0, 0, z)

    def copy_y(i, tt):
        return remote(fb.at[i], ob.at[z], y_ss.at[i, tt], y_rs.at[t, i], (chunk(i, t), e, tt))

    def combine(i):
        take(sor.at[i], q_rs.at[i])
        shared = sac[i] + sor[i]
        take(rr.at[i, pl.ds(0, (E - 1) * CAP)], r_rs.at[i])
        v = lax.dot_general(
            xw[i], rr[i], (((1,), (0,)), ((), ())), precision=lax.Precision.HIGHEST, preferred_element_type=F32
        )
        fb[i] = (v + shared).astype(BF16)

    for i in range(H - 1, -1, -1):
        combine(i)
        copy_y(i, 1).start()
        if i > 0:
            copy_y(i, 0).start()
        else:

            @pl.when(t == 1)
            def _():
                copy_y(0, 0).start()

            @pl.when(t == 0)
            def _():
                ob[z] = fb[0]

    for src in range(2):
        for i in range(H):
            if src == 0 and i == 0:

                @pl.when(t == 1)
                def _():
                    take(ob.at[0], y_rs.at[0, 0])

            else:
                take(ob.at[0], y_rs.at[src, i])
    for d in range(Z):
        out_ref[:, d * B : (d + 1) * B] = ob[d, 0:T, :]

    def sent_a(i):
        copy_a(i, 0).wait_send()
        copy_a(i, 1).wait_send()
        copy_w(i).wait_send()

    for i in range(H):
        take(pk.at[i, pl.ds(0, (E - 1) * CAP)], b_ss.at[i])
        take(oo.at[i, pl.ds(0, (E - 1) * CAP)], r_ss.at[i])
        forward(i).wait_send()
        copy_o(i).wait_send()
        copy_q(i).wait_send()
        copy_y(i, 1).wait_send()
        if i > 0:
            copy_y(i, 0).wait_send()
            sent_a(i)

    @pl.when(t == 1)
    def _():
        copy_y(0, 0).wait_send()
        sent_a(0)

    for k in range(H):
        for half in range(2):
            for way in range(2):
                if k > 0 or half == way:
                    copy_d(way, k, half).wait_send()
                    for q in range(2):
                        copy_c(way, k, half, q).wait_send()
                if k < H - 1 or half == way:
                    copy_g(way, half, k).wait_send()
                    copy_h(way, half, k).wait_send()


def solution(mesh):
    Z, E = mesh.shape["dp"], mesh.shape["expert"]
    H, NS = Z // 2, E * CAP

    def per_device(tokens, ids, rw, wg, wu, wd, sg, su, sd):
        T, D = tokens.shape
        B, F = sg.shape
        FH = F // 2
        dma = pltpu.SemaphoreType.DMA
        vm = pl.BlockSpec(memory_space=pltpu.VMEM)
        hbm = pl.BlockSpec(memory_space=pl.ANY)
        return pl.pallas_call(
            functools.partial(layer_kernel, Z, E, T, B, FH),
            out_shape=jax.ShapeDtypeStruct((T, D), BF16),
            in_specs=[vm] * 2 + [hbm] * 7,
            out_specs=vm,
            scratch_shapes=[
                pltpu.VMEM((B, F), BF16),
                pltpu.VMEM((B, F), BF16),
                pltpu.VMEM((F, B), BF16),
                pltpu.VMEM((B, F), BF16),
                pltpu.VMEM((B, F), BF16),
                pltpu.VMEM((F, B), BF16),
                pltpu.VMEM((T, D), BF16),
                pltpu.VMEM((Z, TP, B), BF16),
                pltpu.VMEM((TP, NS), F32),
                pltpu.VMEM((Z, TP, B), BF16),
                pltpu.VMEM((H, TP, NS), F32),
                pltpu.VMEM((H, NS, B), BF16),
                pltpu.VMEM((Z, NS, B), BF16),
                pltpu.VMEM((2, 2, NS, FH), F32),
                pltpu.VMEM((2, H, 2, 2, NS, FH), BF16),
                pltpu.VMEM((2, H, 2, 2, NS, FH), BF16),
                pltpu.VMEM((2, H, 2, TP, F), BF16),
                pltpu.VMEM((2, H, 2, TP, F), BF16),
                pltpu.VMEM((Z, 2, NS, FH), BF16),
                pltpu.VMEM((Z, 2, TP, FH), BF16),
                pltpu.VMEM((H, NS, B), F32),
                pltpu.VMEM((H, NS, B), F32),
                pltpu.VMEM((H, NS, B), F32),
                pltpu.VMEM((H, TP, B), F32),
                pltpu.VMEM((H, TP, B), F32),
                pltpu.VMEM((H, TP, B), F32),
                pltpu.VMEM((H, NS, B), F32),
                pltpu.VMEM((H, NS, B), F32),
                pltpu.VMEM((H, TP, B), BF16),
                pltpu.VMEM((Z, TP, B), BF16),
                dma((6,)), dma(()),
                dma((H, 2)), dma((2, H)), dma((H,)), dma((H,)), dma((H,)), dma((H,)), dma((H,)), dma((H,)),
                dma((2, H, 2, 2)), dma((2, H, 2, 2)), dma((2, H, 2)), dma((2, H, 2)),
                dma((2, 2, H)), dma((2, 2, H)), dma((2, 2, H)), dma((2, 2, H)),
                dma((H,)), dma((H,)), dma((H,)), dma((H,)), dma((H,)), dma((H,)), dma((H, 2)), dma((2, H)),
            ],
            compiler_params=pltpu.CompilerParams(
                collective_id=0, has_side_effects=True, vmem_limit_bytes=60 * 1024 * 1024
            ),
            name="moe_layer",
        )(ids.T, rw.T, tokens, wg.reshape(wg.shape[1:]), wu.reshape(wu.shape[1:]), wd.reshape(wd.shape[1:]), sg, su, sd)

    placed = (
        P(("dp", "expert"), None),
        P(("dp", "expert"), None),
        P(("dp", "expert"), None),
        P("expert", "dp", "tensor"),
        P("expert", "dp", "tensor"),
        P("expert", "tensor", "dp"),
        P("dp", "tensor"),
        P("dp", "tensor"),
        P("tensor", "dp"),
    )
    return jax.shard_map(
        per_device, mesh=mesh, in_specs=placed, out_specs=P(("dp", "expert"), None), check_vma=False
    )
```

profile of v0, /device:TPU:1, one launch (start us, length us, event | category | flops | bytes accessed | tf_op | source)
XLA Modules:
  0.0 107.2 jit_solution(9237306226104694480)
XLA Ops:
  0.0 105.5 %moe_layer.1 = bf16[12,7168]{1,0:T(8,128)(2,1)} custom-call(s32[8,12]{1,0:T(8,128)} %bitcast.8, f32[8,12]{1,0:T(8,128)} %bitcast.9, bf16[12,7168]{1,0:T(8,128)(2,1)} %tok_hbm.1, bf16[896,1024]{1,0:T(8,128)(2,1)} %bitcast.5, bf16[896,1024]{1,0:T(8,128)(2,1)} %bitcast.6, bf16[1024,896]{1,0:T(8,128)(2,1)} %bitcast.7, bf16[896,1024]{1,0:T(8,128)(2,1)} %sg_hbm.1, ...), custom_call_target="tpu_custom_call" | custom-call | tf_op jit(solution)/shard_map/moe_layer/pallas_call | solution.py:485
  105.5 1.6 %copy.11 = bf16[12,7168]{1,0:T(8,128)(2,1)} copy(bf16[12,7168]{1,0:T(8,128)(2,1)} %moe_layer.1) | data formatting | bytes 344064
where the time goes:
time: 107 us
  Pallas kernels  106 us (99%)
  local copies, waits for them, and re-layouts  1.64 us (2%)
    pallas_call x1, Pallas kernels, per_device(): pl.pallas_call(functools.partial(layer_kernel, Z, E, T, B, FH), out_shape...  106 us

commit v1 on v0

--- a/solution.py
+++ b/solution.py
@@ -24,7 +24,7 @@
     out_ref,
     wg, wu, wd, sg, su, sd,
     tok, tb, tw, xs, xw, pk, x, p, sb, rb, ssb, srb, hid, hs, acc, os_, orc, sac, sos, sor, oo, rr, fb, ob,
-    l_sem, t_sem, a_ss, a_rs, w_ss, w_rs, b_ss, b_rs, f_ss, f_rs,
+    l_sem, t_sem, a_ss, a_rs, v_ss, v_rs, w_ss, w_rs, b_ss, b_rs, f_ss, f_rs,
     c_ss, c_rs, d_ss, d_rs, g_ss, g_rs, h_ss, h_rs, o_ss, o_rs, q_ss, q_rs, r_ss, r_rs, y_ss, y_rs,
 ):
     H = Z // 2
@@ -90,8 +90,10 @@
     before = jnp.zeros((NS, T), F32)
     for r in range(T - 1):
         before = before + jnp.where(token > r, m[:, r : r + 1], 0.0)
-    placed = jnp.where(before == (slot & 7).astype(F32), weight, 0.0)
-    tw[...] = jnp.concatenate([placed, jnp.zeros((NS, NS - T), F32)], axis=1).T[0:TP, :]
+    placed = jnp.where(before == (slot & 7).astype(F32), m, 0.0)
+    which = jnp.sum(placed * (token + 1).astype(F32), axis=1, keepdims=True) - 1.0
+    weight = jnp.sum(placed * weight, axis=1, keepdims=True)
+    tw[...] = jnp.concatenate([which, weight, jnp.zeros((NS, NS - 2), F32)], axis=1).T[0:8, :]
     for d in range(Z):
         tb[d, 8:TP, :] = jnp.zeros((TP - 8, B), BF16)
     tok_load.wait()
@@ -102,23 +104,27 @@
 
     pl.semaphore_wait(barrier, 2 * (Z - 1) + (E - 1) + 1)
 
-    def target_a(i):
-        return lax.rem(z + (1 - t) * i + t * (Z - 1 - i), Z)
-
-    def copy_a(i, tt):
-        return remote(tb.at[target_a(i)], xs.at[z], a_ss.at[i, tt], a_rs.at[t, i], (target_a(i), e, tt))
-
-    def copy_w(i):
-        return remote(tw, xw.at[i], w_ss.at[i], w_rs.at[i], (target_a(i), e, t))
+    def copies_a(i):
+        d = lax.rem(z + (1 - t) * i + t * (Z - 1 - i), Z)
+        return (
+            remote(tw, xw.at[i], w_ss.at[i], w_rs.at[i], (d, e, t)),
+            remote(tb.at[d], xs.at[z], a_ss.at[i], a_rs.at[i], (d, e, t)),
+        )
 
     def start_a(i):
-        copy_a(i, 0).start()
-        copy_a(i, 1).start()
-        copy_w(i).start()
+        for c in copies_a(i):
+            c.start()
+
+    def copy_v(i):
+        c = chunk(i, t)
+        return remote(xs.at[c], xs.at[c], v_ss.at[i], v_rs.at[i], (z, e, pt))
+
+    def named_by(i):
+        return lax.broadcasted_iota(jnp.int32, (TP, NS), 0).astype(F32) == xw[i, 0:1, :]
 
     def pick(i):
         zc = chunk(i, t)
-        cb = jnp.where(xw[i] > 0.0, 1.0, 0.0).astype(BF16)
+        cb = jnp.where(named_by(i), 1.0, 0.0).astype(BF16)
         picked = lax.dot_general(cb, xs[zc], (((0,), (0,)), ((), ())), preferred_element_type=F32)
         pk[i] = picked.astype(BF16)
 
@@ -130,6 +136,12 @@
         lax.fori_loop(1, E, send_b, 0)
         x[zc, rows(e), :] = pk[i, rows(e), :]
 
+    def arrive(i):
+        take(xw.at[i], w_rs.at[i])
+        take(xs.at[0], a_rs.at[i])
+        copy_v(i).start()
+        pick(i)
+
     def copy_d(way, k, half):
         return remote(
             ssb.at[way, k, half], srb.at[way, k, half], d_ss.at[way, k, half], d_rs.at[way, k, half], next_to(way)
@@ -138,18 +150,21 @@
     def cols(half):
         return slice(half * FH, (half + 1) * FH)
 
-    def step_s(k):
+    def step_s(k, first):
+        if first > 0:
+            take(xs.at[0], v_rs.at[k - pt])
         for half in range(2):
-            ways = (half,) if k == 0 else (0, 1)
+            ways = (half,) if first == 0 else (0, 1)
             v = [xs[at(way, k)] for way in ways]
-            v = v[0] if k == 0 else jnp.concatenate(v, axis=0)
+            v = v[0] if first == 0 else jnp.concatenate(v, axis=0)
             sums = [dot(v, w[:, cols(half)]) for w in (sg, su)]
             for n, way in enumerate(ways):
-                if k > 1 or (k == 1 and half == way):
+                add = first > 1 or (first == 1 and half == way)
+                if add:
                     copy_d(way, k - 1, half).wait_recv()
                 for q in range(2):
                     u = sums[q][n * TP : (n + 1) * TP]
-                    if k > 1 or (k == 1 and half == way):
+                    if add:
                         u = u + srb[way, k - 1, half, :, cols(q)].astype(F32)
                     ssb[way, k, half, :, cols(q)] = u.astype(BF16)
                 copy_d(way, k, half).start()
@@ -158,6 +173,10 @@
         return (g / (1.0 + jnp.exp(-g)) * u).astype(BF16)
 
     def last_s():
+        @pl.when(t == 0)
+        def _():
+            take(xs.at[0], v_rs.at[H - 1])
+
         for half in range(2):
             for way in range(2):
                 copy_d(way, H - 1, half).wait_recv()
@@ -184,23 +203,8 @@
 
     for load in loads[:2]:
         load.wait()
-    step_s(0)
-    for k in range(1, H):
-        take(xs.at[0], a_rs.at[0, k])
-        take(xs.at[0], a_rs.at[1, k - 1])
-        take(xw.at[0], w_rs.at[k - t])
-        pick(k - t)
-        if k == 1 and H > 2:
-            step_s(1)
-    take(xs.at[0], a_rs.at[1, H - 1])
-
-    @pl.when(t == 1)
-    def _():
-        take(xw.at[0], w_rs.at[H - 1])
-        pick(H - 1)
-
-    for k in range(2, H - 1):
-        step_s(k)
+    step_s(0, 0)
+    arrive(1 - t)
     for load in loads[2:4]:
         load.wait()
 
@@ -240,7 +244,14 @@
             partial(z, way, q, way)
             sb[way, 0, way, q] = p[way, q].astype(BF16)
             copy_c(way, 0, way, q).start()
-    step_s(H - 1)
+    for k in range(2, H):
+        arrive(k - t)
+
+    @pl.when(t == 1)
+    def _():
+        arrive(H - 1)
+
+    step_s(1, 1)
 
     def step_c(k, carry):
         pass_on(k - t)
@@ -260,6 +271,11 @@
                         pl.when(k > 1)(plus)
                     sb[way, k, half, q] = p[way, q].astype(BF16)
                     copy_c(way, k, half, q).start()
+
+        @pl.when(k < H - 1)
+        def _():
+            step_s(k + 1, 2)
+
         return carry
 
     lax.fori_loop(1, H, step_c, 0)
@@ -406,7 +422,7 @@
         shared = sac[i] + sor[i]
         take(rr.at[i, pl.ds(0, (E - 1) * CAP)], r_rs.at[i])
         v = lax.dot_general(
-            xw[i], rr[i], (((1,), (0,)), ((), ())), precision=lax.Precision.HIGHEST, preferred_element_type=F32
+            jnp.where(named_by(i), xw[i, 1:2, :], 0.0), rr[i], (((1,), (0,)), ((), ())), precision=lax.Precision.HIGHEST, preferred_element_type=F32
         )
         fb[i] = (v + shared).astype(BF16)
 
@@ -439,9 +455,9 @@
         out_ref[:, d * B : (d + 1) * B] = ob[d, 0:T, :]
 
     def sent_a(i):
-        copy_a(i, 0).wait_send()
-        copy_a(i, 1).wait_send()
-        copy_w(i).wait_send()
+        for c in copies_a(i):
+            c.wait_send()
+        copy_v(i).wait_send()
 
     for i in range(H):
         take(pk.at[i, pl.ds(0, (E - 1) * CAP)], b_ss.at[i])
@@ -496,9 +512,9 @@
                 pltpu.VMEM((F, B), BF16),
                 pltpu.VMEM((T, D), BF16),
                 pltpu.VMEM((Z, TP, B), BF16),
-                pltpu.VMEM((TP, NS), F32),
+                pltpu.VMEM((8, NS), F32),
                 pltpu.VMEM((Z, TP, B), BF16),
-                pltpu.VMEM((H, TP, NS), F32),
+                pltpu.VMEM((H, 8, NS), F32),
                 pltpu.VMEM((H, NS, B), BF16),
                 pltpu.VMEM((Z, NS, B), BF16),
                 pltpu.VMEM((2, 2, NS, FH), F32),
@@ -519,7 +535,7 @@
                 pltpu.VMEM((H, TP, B), BF16),
                 pltpu.VMEM((Z, TP, B), BF16),
                 dma((6,)), dma(()),
-                dma((H, 2)), dma((2, H)), dma((H,)), dma((H,)), dma((H,)), dma((H,)), dma((H,)), dma((H,)),
+                dma((H,)), dma((H,)), dma((H,)), dma((H,)), dma((H,)), dma((H,)), dma((H,)), dma((H,)), dma((H,)), dma((H,)),
                 dma((2, H, 2, 2)), dma((2, H, 2, 2)), dma((2, H, 2)), dma((2, H, 2)),
                 dma((2, 2, H)), dma((2, 2, H)), dma((2, 2, H)), dma((2, 2, H)),
                 dma((H,)), dma((H,)), dma((H,)), dma((H,)), dma((H,)), dma((H,)), dma((H, 2)), dma((2, H)),

time: 107 us -> 103 us (0.963)
  Pallas kernels: 106 us -> 101 us
    pallas_call x1, Pallas kernels: 106 us -> 101 us  [per_device(): pl.pallas_call(functools.partial(layer_kernel, Z, E, T, B, FH), out_shape...]
where the time goes in v1:
time: 103 us; the launch traced here: 102 us
  Pallas kernels  101 us (98%)
  local copies, waits for them, and re-layouts  1.64 us (2%)
    pallas_call x1, Pallas kernels, per_device(): pl.pallas_call(functools.partial(layer_kernel, Z, E, T, B, FH), out_shape...  101 us

profile of v1, /device:TPU:1, one launch (start us, length us, event | category | flops | bytes accessed | tf_op | source)
XLA Modules:
  0.0 102.4 jit_solution(6926252237868615650)
XLA Ops:
  0.0 100.7 %moe_layer.1 = bf16[12,7168]{1,0:T(8,128)(2,1)} custom-call(s32[8,12]{1,0:T(8,128)} %bitcast.8, f32[8,12]{1,0:T(8,128)} %bitcast.9, bf16[12,7168]{1,0:T(8,128)(2,1)} %tok_hbm.1, bf16[896,1024]{1,0:T(8,128)(2,1)} %bitcast.5, bf16[896,1024]{1,0:T(8,128)(2,1)} %bitcast.6, bf16[1024,896]{1,0:T(8,128)(2,1)} %bitcast.7, bf16[896,1024]{1,0:T(8,128)(2,1)} %sg_hbm.1, ...), custom_call_target="tpu_custom_call" | custom-call | tf_op jit(solution)/shard_map/moe_layer/pallas_call | solution.py:501
  100.7 1.6 %copy.11 = bf16[12,7168]{1,0:T(8,128)(2,1)} copy(bf16[12,7168]{1,0:T(8,128)(2,1)} %moe_layer.1) | data formatting | bytes 344064

commit v2 on v1

--- a/solution.py
+++ b/solution.py
@@ -16,6 +16,22 @@
 
 def dot(a, b):
     return jnp.dot(a, b, preferred_element_type=F32)
+
+
+CODES = 237.0
+LOWEST = 126.0
+LOG2E = 1.4426950408889634
+
+
+def code(v):
+    c = jnp.maximum((jnp.log(jnp.abs(v)) * LOG2E + LOWEST) * CODES + 0.5, 0.0).astype(jnp.int32)
+    return jnp.where(v < 0.0, -c, c).astype(jnp.int16)
+
+
+def value(coded):
+    c = coded.astype(jnp.int32)
+    v = jnp.exp2(jnp.abs(c).astype(F32) * (1.0 / CODES) - LOWEST)
+    return jnp.where(c > 0, v, jnp.where(c < 0, -v, 0.0))
 
 
 def layer_kernel(
@@ -150,6 +166,9 @@
     def cols(half):
         return slice(half * FH, (half + 1) * FH)
 
+    def pack(g, u):
+        return jnp.concatenate([g[0:8], u[0:8], g[8:T], u[8:T]], axis=0)
+
     def step_s(k, first):
         if first > 0:
             take(xs.at[0], v_rs.at[k - pt])
@@ -162,11 +181,10 @@
                 add = first > 1 or (first == 1 and half == way)
                 if add:
                     copy_d(way, k - 1, half).wait_recv()
-                for q in range(2):
-                    u = sums[q][n * TP : (n + 1) * TP]
-                    if add:
-                        u = u + srb[way, k - 1, half, :, cols(q)].astype(F32)
-                    ssb[way, k, half, :, cols(q)] = u.astype(BF16)
+                packed = pack(*[u[n * TP : (n + 1) * TP] for u in sums])
+                if add:
+                    packed = packed + value(srb[way, k - 1, half])
+                ssb[way, k, half] = code(packed)
                 copy_d(way, k, half).start()
 
     def silu_up(g, u):
@@ -180,12 +198,11 @@
         for half in range(2):
             for way in range(2):
                 copy_d(way, H - 1, half).wait_recv()
-            g, u = [
-                dot(xs[far], w[:, cols(half)])
-                + srb[0, H - 1, half, :, cols(q)].astype(F32)
-                + srb[1, H - 1, half, :, cols(q)].astype(F32)
-                for q, w in enumerate((sg, su))
-            ]
+            m = pack(dot(xs[far], sg[:, cols(half)]), dot(xs[far], su[:, cols(half)]))
+            m = m + value(srb[0, H - 1, half]) + value(srb[1, H - 1, half])
+            rest = jnp.zeros((TP - T, FH), F32)
+            g = jnp.concatenate([m[0:8], m[16 : 8 + T], rest], axis=0)
+            u = jnp.concatenate([m[8:16], m[8 + T : 2 * T], rest], axis=0)
             hs[far, half] = silu_up(g, u)
 
     @pl.when(t == 1)
@@ -242,7 +259,7 @@
     for q in range(2):
         for way in range(2):
             partial(z, way, q, way)
-            sb[way, 0, way, q] = p[way, q].astype(BF16)
+            sb[way, 0, way, q] = code(p[way, q])
             copy_c(way, 0, way, q).start()
     for k in range(2, H):
         arrive(k - t)
@@ -263,13 +280,13 @@
 
                     def plus(half=half, q=q, way=way):
                         copy_c(way, k - 1, half, q).wait_recv()
-                        p[way, q] = p[way, q] + rb[way, k - 1, half, q].astype(F32)
+                        p[way, q] = p[way, q] + value(rb[way, k - 1, half, q])
 
                     if half == way:
                         plus()
                     else:
                         pl.when(k > 1)(plus)
-                    sb[way, k, half, q] = p[way, q].astype(BF16)
+                    sb[way, k, half, q] = code(p[way, q])
                     copy_c(way, k, half, q).start()
 
         @pl.when(k < H - 1)
@@ -311,7 +328,7 @@
         for q in range(2):
             for way in range(2):
                 copy_c(way, H - 1, half, q).wait_recv()
-            p[half, q] = p[half, q] + rb[0, H - 1, half, q].astype(F32) + rb[1, H - 1, half, q].astype(F32)
+            p[half, q] = p[half, q] + value(rb[0, H - 1, half, q]) + value(rb[1, H - 1, half, q])
         hid[far, half] = silu_up(p[half, 0], p[half, 1])
         for way in range(2):
             copy_g(way, half, 0).start()
@@ -335,7 +352,7 @@
 
         @pl.when(t != keeper)
         def _():
-            os_[i] = down(hid[c], wd)
+            os_[i] = down(hid[c], wd).astype(BF16)
             copy_o(i).start()
 
     def shared_one(i, keeper, c):
@@ -359,7 +376,7 @@
 
     def finish(i):
         copy_o(i).wait_recv()
-        oo[i] = acc[i] + orc[i]
+        oo[i] = (acc[i] + orc[i].astype(F32)).astype(BF16)
 
         def send_r(k, carry):
             ee = lax.rem(e + k, E)
@@ -379,15 +396,15 @@
             finish(mine + 1)
         for way in range(2):
             hop(copy_g, way, 1, j)
+        os_[theirs] = down(hid[chunk(theirs, pt)], wd).astype(BF16)
+        copy_o(theirs).start()
+        acc[mine] = down(hid[chunk(mine, t)], wd)
         for half in range(2):
             for way in range(2):
                 if j == 1:
                     copy_h(way, half, 0).start()
                 else:
                     hop(copy_h, way, half, j - 1)
-        os_[theirs] = down(hid[chunk(theirs, pt)], wd)
-        copy_o(theirs).start()
-        acc[mine] = down(hid[chunk(mine, t)], wd)
         if j == 1:
             shared_one(H - 1, 1, far)
 
@@ -422,7 +439,11 @@
         shared = sac[i] + sor[i]
         take(rr.at[i, pl.ds(0, (E - 1) * CAP)], r_rs.at[i])
         v = lax.dot_general(
-            jnp.where(named_by(i), xw[i, 1:2, :], 0.0), rr[i], (((1,), (0,)), ((), ())), precision=lax.Precision.HIGHEST, preferred_element_type=F32
+            jnp.where(named_by(i), xw[i, 1:2, :], 0.0),
+            rr[i].astype(F32),
+            (((1,), (0,)), ((), ())),
+            precision=lax.Precision.HIGHEST,
+            preferred_element_type=F32,
         )
         fb[i] = (v + shared).astype(BF16)
 
@@ -518,20 +539,20 @@
                 pltpu.VMEM((H, NS, B), BF16),
                 pltpu.VMEM((Z, NS, B), BF16),
                 pltpu.VMEM((2, 2, NS, FH), F32),
-                pltpu.VMEM((2, H, 2, 2, NS, FH), BF16),
-                pltpu.VMEM((2, H, 2, 2, NS, FH), BF16),
-                pltpu.VMEM((2, H, 2, TP, F), BF16),
-                pltpu.VMEM((2, H, 2, TP, F), BF16),
+                pltpu.VMEM((2, H, 2, 2, NS, FH), jnp.int16),
+                pltpu.VMEM((2, H, 2, 2, NS, FH), jnp.int16),
+                pltpu.VMEM((2, H, 2, 2 * T, FH), jnp.int16),
+                pltpu.VMEM((2, H, 2, 2 * T, FH), jnp.int16),
                 pltpu.VMEM((Z, 2, NS, FH), BF16),
                 pltpu.VMEM((Z, 2, TP, FH), BF16),
                 pltpu.VMEM((H, NS, B), F32),
-                pltpu.VMEM((H, NS, B), F32),
-                pltpu.VMEM((H, NS, B), F32),
+                pltpu.VMEM((H, NS, B), BF16),
+                pltpu.VMEM((H, NS, B), BF16),
                 pltpu.VMEM((H, TP, B), F32),
                 pltpu.VMEM((H, TP, B), F32),
                 pltpu.VMEM((H, TP, B), F32),
-                pltpu.VMEM((H, NS, B), F32),
-                pltpu.VMEM((H, NS, B), F32),
+                pltpu.VMEM((H, NS, B), BF16),
+                pltpu.VMEM((H, NS, B), BF16),
                 pltpu.VMEM((H, TP, B), BF16),
                 pltpu.VMEM((Z, TP, B), BF16),
                 dma((6,)), dma(()),

time: 103 us -> 101 us (0.981)
  Pallas kernels: 101 us -> 98.7 us
    pallas_call x1, Pallas kernels: 101 us -> 98.7 us  [per_device(): pl.pallas_call(functools.partial(layer_kernel, Z, E, T, B, FH), out_shape...]
where the time goes in v2:
time: 101 us; the launch traced here: 100 us
  Pallas kernels  98.7 us (98%)
  local copies, waits for them, and re-layouts  1.64 us (2%)
    pallas_call x1, Pallas kernels, per_device(): pl.pallas_call(functools.partial(layer_kernel, Z, E, T, B, FH), out_shape...  98.7 us

profile of v2, /device:TPU:1, one launch (start us, length us, event | category | flops | bytes accessed | tf_op | source)
XLA Modules:
  0.0 100.4 jit_solution(9362043913001475893)
XLA Ops:
  0.0 98.7 %moe_layer.1 = bf16[12,7168]{1,0:T(8,128)(2,1)} custom-call(s32[8,12]{1,0:T(8,128)} %bitcast.8, f32[8,12]{1,0:T(8,128)} %bitcast.9, bf16[12,7168]{1,0:T(8,128)(2,1)} %tok_hbm.1, bf16[896,1024]{1,0:T(8,128)(2,1)} %bitcast.5, bf16[896,1024]{1,0:T(8,128)(2,1)} %bitcast.6, bf16[1024,896]{1,0:T(8,128)(2,1)} %bitcast.7, bf16[896,1024]{1,0:T(8,128)(2,1)} %sg_hbm.1, ...), custom_call_target="tpu_custom_call" | custom-call | tf_op jit(solution)/shard_map/moe_layer/pallas_call | solution.py:522
  98.7 1.6 %copy.11 = bf16[12,7168]{1,0:T(8,128)(2,1)} copy(bf16[12,7168]{1,0:T(8,128)(2,1)} %moe_layer.1) | data formatting | bytes 344064

commit v3 on v2

--- a/solution.py
+++ b/solution.py
@@ -325,6 +325,9 @@
             partial(far, half, q, half)
     last_s()
     for half in range(2):
+        for way in range(2):
+            copy_h(way, half, 0).start()
+    for half in range(2):
         for q in range(2):
             for way in range(2):
                 copy_c(way, H - 1, half, q).wait_recv()
@@ -386,7 +389,39 @@
         lax.fori_loop(1, E, send_r, 0)
         rr[i, rows(e), :] = oo[i, rows(e), :]
 
+    def copy_y(i, tt):
+        return remote(fb.at[i], ob.at[z], y_ss.at[i, tt], y_rs.at[t, i], (chunk(i, t), e, tt))
+
+    def combine(i):
+        take(sor.at[i], q_rs.at[i])
+        shared = sac[i] + sor[i]
+        take(rr.at[i, pl.ds(0, (E - 1) * CAP)], r_rs.at[i])
+        v = lax.dot_general(
+            jnp.where(named_by(i), xw[i, 1:2, :], 0.0),
+            rr[i].astype(F32),
+            (((1,), (0,)), ((), ())),
+            precision=lax.Precision.HIGHEST,
+            preferred_element_type=F32,
+        )
+        fb[i] = (v + shared).astype(BF16)
+
+    def go_home(i):
+        combine(i)
+        copy_y(i, 1).start()
+        if i > 0:
+            copy_y(i, 0).start()
+        else:
+
+            @pl.when(t == 1)
+            def _():
+                copy_y(0, 0).start()
+
+            @pl.when(t == 0)
+            def _():
+                ob[z] = fb[0]
+
     keep_or_give(H - 1, 1, far)
+    shared_one(H - 1, 1, far)
     for j in range(1, H):
         mine = H - j - t
         theirs = H - j - pt
@@ -401,66 +436,30 @@
         acc[mine] = down(hid[chunk(mine, t)], wd)
         for half in range(2):
             for way in range(2):
-                if j == 1:
-                    copy_h(way, half, 0).start()
-                else:
-                    hop(copy_h, way, half, j - 1)
+                hop(copy_h, way, half, j)
         if j == 1:
-            shared_one(H - 1, 1, far)
 
             @pl.when(t == 1)
             def _():
                 finish(H - 1)
 
-        else:
-            shared_pair(theirs + 1, mine + 1)
+        shared_pair(theirs, mine)
     finish(1 - t)
-    for half in range(2):
-        for way in range(2):
-            hop(copy_h, way, half, H - 1)
+    if H > 2:
+        go_home(H - 1)
     copy_g(0, 0, H - 1).wait_recv()
     copy_g(1, 1, H - 1).wait_recv()
     keep_or_give(0, 0, z)
-    shared_pair(1 - pt, 1 - t)
-
-    @pl.when(t == 0)
-    def _():
-        finish(0)
-
     copy_h(0, 0, H - 1).wait_recv()
     copy_h(1, 1, H - 1).wait_recv()
     shared_one(0, 0, z)
 
-    def copy_y(i, tt):
-        return remote(fb.at[i], ob.at[z], y_ss.at[i, tt], y_rs.at[t, i], (chunk(i, t), e, tt))
-
-    def combine(i):
-        take(sor.at[i], q_rs.at[i])
-        shared = sac[i] + sor[i]
-        take(rr.at[i, pl.ds(0, (E - 1) * CAP)], r_rs.at[i])
-        v = lax.dot_general(
-            jnp.where(named_by(i), xw[i, 1:2, :], 0.0),
-            rr[i].astype(F32),
-            (((1,), (0,)), ((), ())),
-            precision=lax.Precision.HIGHEST,
-            preferred_element_type=F32,
-        )
-        fb[i] = (v + shared).astype(BF16)
-
-    for i in range(H - 1, -1, -1):
-        combine(i)
-        copy_y(i, 1).start()
-        if i > 0:
-            copy_y(i, 0).start()
-        else:
-
-            @pl.when(t == 1)
-            def _():
-                copy_y(0, 0).start()
-
-            @pl.when(t == 0)
-            def _():
-                ob[z] = fb[0]
+    @pl.when(t == 0)
+    def _():
+        finish(0)
+
+    for i in range(H - 1 if H == 2 else H - 2, -1, -1):
+        go_home(i)
 
     for src in range(2):
         for i in range(H):

time: 101 us -> 99.2 us (0.982)
  Pallas kernels: 98.7 us -> 97.3 us
    pallas_call x1, Pallas kernels: 98.7 us -> 97.3 us  [per_device(): pl.pallas_call(functools.partial(layer_kernel, Z, E, T, B, FH), out_shape...]
where the time goes in v3:
time: 99.2 us; the launch traced here: 99 us
  Pallas kernels  97.3 us (98%)
  local copies, waits for them, and re-layouts  1.64 us (2%)
    pallas_call x1, Pallas kernels, per_device(): pl.pallas_call(functools.partial(layer_kernel, Z, E, T, B, FH), out_shape...  97.3 us

profile of v3, /device:TPU:1, one launch (start us, length us, event | category | flops | bytes accessed | tf_op | source)
XLA Modules:
  0.0 99.0 jit_solution(15408805620080114576)
XLA Ops:
  0.0 97.3 %moe_layer.1 = bf16[12,7168]{1,0:T(8,128)(2,1)} custom-call(s32[8,12]{1,0:T(8,128)} %bitcast.8, f32[8,12]{1,0:T(8,128)} %bitcast.9, bf16[12,7168]{1,0:T(8,128)(2,1)} %tok_hbm.1, bf16[896,1024]{1,0:T(8,128)(2,1)} %bitcast.5, bf16[896,1024]{1,0:T(8,128)(2,1)} %bitcast.6, bf16[1024,896]{1,0:T(8,128)(2,1)} %bitcast.7, bf16[896,1024]{1,0:T(8,128)(2,1)} %sg_hbm.1, ...), custom_call_target="tpu_custom_call" | custom-call | tf_op jit(solution)/shard_map/moe_layer/pallas_call | solution.py:521
  97.3 1.6 %copy.11 = bf16[12,7168]{1,0:T(8,128)(2,1)} copy(bf16[12,7168]{1,0:T(8,128)(2,1)} %moe_layer.1) | data formatting | bytes 344064

commit v4 on v3

--- a/solution.py
+++ b/solution.py
@@ -205,23 +205,24 @@
             u = jnp.concatenate([m[8:16], m[8 + T : 2 * T], rest], axis=0)
             hs[far, half] = silu_up(g, u)
 
+    xs[z] = tb[z]
+
+    @pl.when(t == 0)
+    def _():
+        xw[0] = tw[...]
+        pick(0)
+
     @pl.when(t == 1)
     def _():
         start_a(0)
 
     for i in range(1, H):
         start_a(i)
-    xs[z] = tb[z]
-
-    @pl.when(t == 0)
-    def _():
-        xw[0] = tw[...]
-        pick(0)
-
     for load in loads[:2]:
         load.wait()
     step_s(0, 0)
     arrive(1 - t)
+    step_s(1, 1)
     for load in loads[2:4]:
         load.wait()
 
@@ -267,8 +268,6 @@
     @pl.when(t == 1)
     def _():
         arrive(H - 1)
-
-    step_s(1, 1)
 
     def step_c(k, carry):
         pass_on(k - t)

time: 99.2 us -> 98.7 us (level)
  Pallas kernels: 97.3 us -> 96.3 us
    pallas_call x1, Pallas kernels: 97.3 us -> 96.3 us  [per_device(): pl.pallas_call(functools.partial(layer_kernel, Z, E, T, B, FH), out_shape...]
where the time goes in v4:
time: 98.7 us; the launch traced here: 97.9 us
  Pallas kernels  96.3 us (98%)
  local copies, waits for them, and re-layouts  1.64 us (2%)
    pallas_call x1, Pallas kernels, per_device(): pl.pallas_call(functools.partial(layer_kernel, Z, E, T, B, FH), out_shape...  96.3 us

profile of v4, /device:TPU:1, one launch (start us, length us, event | category | flops | bytes accessed | tf_op | source)
XLA Modules:
  0.0 97.9 jit_solution(17381270447895030414)
XLA Ops:
  0.0 96.3 %moe_layer.1 = bf16[12,7168]{1,0:T(8,128)(2,1)} custom-call(s32[8,12]{1,0:T(8,128)} %bitcast.8, f32[8,12]{1,0:T(8,128)} %bitcast.9, bf16[12,7168]{1,0:T(8,128)(2,1)} %tok_hbm.1, bf16[896,1024]{1,0:T(8,128)(2,1)} %bitcast.5, bf16[896,1024]{1,0:T(8,128)(2,1)} %bitcast.6, bf16[1024,896]{1,0:T(8,128)(2,1)} %bitcast.7, bf16[896,1024]{1,0:T(8,128)(2,1)} %sg_hbm.1, ...), custom_call_target="tpu_custom_call" | custom-call | tf_op jit(solution)/shard_map/moe_layer/pallas_call | solution.py:520
  96.3 1.6 %copy.11 = bf16[12,7168]{1,0:T(8,128)(2,1)} copy(bf16[12,7168]{1,0:T(8,128)(2,1)} %moe_layer.1) | data formatting | bytes 344064

commit v5 on v4

--- a/solution.py
+++ b/solution.py
@@ -449,13 +449,13 @@
     copy_g(0, 0, H - 1).wait_recv()
     copy_g(1, 1, H - 1).wait_recv()
     keep_or_give(0, 0, z)
+    @pl.when(t == 0)
+    def _():
+        finish(0)
+
     copy_h(0, 0, H - 1).wait_recv()
     copy_h(1, 1, H - 1).wait_recv()
     shared_one(0, 0, z)
-
-    @pl.when(t == 0)
-    def _():
-        finish(0)
 
     for i in range(H - 1 if H == 2 else H - 2, -1, -1):
         go_home(i)

time: 98.7 us -> 98.3 us (level)
  no operation moved by 1% of the time
where the time goes in v5:
time: 98.3 us; the launch traced here: 97.8 us
  Pallas kernels  96.2 us (98%)
  local copies, waits for them, and re-layouts  1.64 us (2%)
    pallas_call x1, Pallas kernels, per_device(): pl.pallas_call(functools.partial(layer_kernel, Z, E, T, B, FH), out_shape...  96.2 us

profile of v5, /device:TPU:1, one launch (start us, length us, event | category | flops | bytes accessed | tf_op | source)
XLA Modules:
  0.0 97.8 jit_solution(16973344984658096586)
XLA Ops:
  0.0 96.2 %moe_layer.1 = bf16[12,7168]{1,0:T(8,128)(2,1)} custom-call(s32[8,12]{1,0:T(8,128)} %bitcast.8, f32[8,12]{1,0:T(8,128)} %bitcast.9, bf16[12,7168]{1,0:T(8,128)(2,1)} %tok_hbm.1, bf16[896,1024]{1,0:T(8,128)(2,1)} %bitcast.5, bf16[896,1024]{1,0:T(8,128)(2,1)} %bitcast.6, bf16[1024,896]{1,0:T(8,128)(2,1)} %bitcast.7, bf16[896,1024]{1,0:T(8,128)(2,1)} %sg_hbm.1, ...), custom_call_target="tpu_custom_call" | custom-call | tf_op jit(solution)/shard_map/moe_layer/pallas_call | solution.py:520
  96.2 1.6 %copy.11 = bf16[12,7168]{1,0:T(8,128)(2,1)} copy(bf16[12,7168]{1,0:T(8,128)(2,1)} %moe_layer.1) | data formatting | bytes 344064
